TPU v7x, 32 devices: a whole 2x2x4 slice. The times are simulated.
32 devices in a mesh: dp: 8 (over z, x), mp: 4 (over y, core).
Axes of the slice: x: 2, y: 2, z: 4, core: 2. Of those that a mesh axis runs over, the one named last changes fastest.
Arguments:
- query_emb: bfloat16 [2048, 768], P('dp'), may hold values from -6 to 6
- positive_list: int32 [2048], replicated, may hold values from 0 to 32767
- centroids: float32 [32768, 768], P(('dp', 'mp')), may hold values from -0.6 to 0.6
- first_moment: float32 [32768, 768], P(('dp', 'mp')), may hold values from -3 to 3
- second_moment: float32 [32768, 768], P(('dp', 'mp')), may hold values from 0.05 to 2
Outputs:
- new_centroids: float32 [32768, 768], P(('dp', 'mp'))
- new_first: float32 [32768, 768], P(('dp', 'mp'))
- new_second: float32 [32768, 768], P(('dp', 'mp'))
- mean_loss: float32 [], replicated
All inputs are finite; a program needn't handle non-finite values.
Results may differ from a plain program's by a relative error of at most 0.00097.
Values may be sent and summed in bfloat16 or wider, within the bound.
A program may use at most 64 MiB of HBM per device.

v0:
```python
import jax
import jax.numpy as jnp
from jax import lax
from jax.sharding import PartitionSpec as P

beta_first = 0.9
beta_second = 0.95
learn_rate = 0.01
epsilon = 1e-08


def adam_update(centroids, first_moment, second_moment, gradient):
    new_first = beta_first * first_moment + (1.0 - beta_first) * gradient
    new_second = beta_second * second_moment + (1.0 - beta_second) * gradient * gradient
    new_centroids = centroids - learn_rate * new_first / (jnp.sqrt(new_second) + epsilon)
    return (new_centroids, new_first, new_second)


def target_logit(logits, is_target):
    return jnp.sum(jnp.where(is_target, logits, jnp.zeros_like(logits)), axis=1)


def row_terms(logits, is_target, row_peak, row_mass, row_target):
    log_norm = row_peak + jnp.log(row_mass)
    row_loss = log_norm - row_target
    weights = (jnp.exp(logits - log_norm[:, None]) - is_target.astype(jnp.float32)).astype(
        jnp.bfloat16
    )
    return (row_loss, weights)


def shards(query_emb, positive_list, centroids, first_moment, second_moment):
    table_half = centroids.astype(jnp.bfloat16)
    own_lists = centroids.shape[0]
    count_mp = lax.axis_size("mp")
    dp_index = lax.axis_index("dp")
    mp_index = lax.axis_index("mp")
    gathered = lax.all_gather(query_emb, "dp", axis=0, tiled=True)
    logits = jnp.einsum("rd,kd->rk", gathered, table_half, preferred_element_type=jnp.float32)
    shard_block = dp_index * count_mp + mp_index
    global_col = shard_block * own_lists + lax.iota(jnp.int32, own_lists)
    is_target = global_col[None, :] == positive_list[:, None]
    row_peak = lax.pmax(jnp.max(logits, axis=1).astype(jnp.bfloat16), ("dp", "mp")).astype(
        jnp.float32
    )
    local_mass = jnp.sum(jnp.exp(logits - row_peak[:, None]), axis=1)
    row_mass, row_target = lax.psum((local_mass, target_logit(logits, is_target)), ("dp", "mp"))
    row_loss, weights = row_terms(logits, is_target, row_peak, row_mass, row_target)
    mean_loss = jnp.mean(row_loss)
    gradient = jnp.einsum("rk,rd->kd", weights, gathered, preferred_element_type=jnp.float32)
    new_centroids, new_first, new_second = adam_update(
        centroids, first_moment, second_moment, gradient
    )
    return (new_centroids, new_first, new_second, mean_loss)


def solution(mesh):
    in_specs = (
        P("dp", None),
        P(),
        P(("dp", "mp"), None),
        P(("dp", "mp"), None),
        P(("dp", "mp"), None),
    )
    out_specs = (P(("dp", "mp"), None), P(("dp", "mp"), None), P(("dp", "mp"), None), P())
    return jax.shard_map(shards, mesh=mesh, in_specs=in_specs, out_specs=out_specs, check_vma=False)
```

profile of v0, /device:TPU:0, one launch (start us, length us, event | category | flops | bytes accessed | tf_op | source)
XLA Modules:
  0.0 188.3 jit_solution(12831864654990041094)
XLA Ops:
  7.2 0.0 all-gather.2.cloned.1.call-start
  7.2 0.7 all-gather.2.cloned.1.call-update
  7.9 0.0 copy-start
  7.9 65.0 %all-gather.2.cloned.1.call-done = bf16[2048,768]{1,0:T(8,128)(2,1)} async-done(((bf16[256,768]{1,0:T(8,128)(2,1)}), bf16[2048,768]{1,0:T(8,128)(2,1)}) %all-gather.2.cloned.1.call-update) | async-done | bytes 3145744 | tf_op jit(solution)/shard_map/all_gather | solution.py:38
  72.9 9.5 %fusion.12 = (bf16[2048]{0:T(1024)(128)(2,1)S(1)}, f32[2048,1024]{0,1:T(8,128)}) fusion(bf16[2048,768]{1,0:T(8,128)(2,1)} %all-gather.2.cloned.1.call-done, f32[1024,768]{1,0:T(8,128)} %param.7), kind=kOutput, calls=%fused_computation.19 | convolution fusion | flops 3224107008 | bytes 14684160 | tf_op jit(solution)/shard_map/rd,kd->rk/dot_general | solution.py:39
  82.4 39.2 %pmax.7 = bf16[2048]{0:T(1024)(128)(2,1)S(1)} all-reduce(bf16[2048]{0:T(1024)(128)(2,1)S(1)} %get-tuple-element.13), channel_id=1, replica_groups=mesh['dp'=8,'mp'=4] {'dp','mp'}, use_global_device_ids=true, to_apply=%region_1.0 | all-reduce | flops 2048 | bytes 8192 | tf_op jit(solution)/shard_map/pmax | solution.py:43
  121.7 0.0 copy-done
  121.7 0.0 copy-start.1
  121.7 4.7 %fusion.2 = (f32[2048]{0:T(1024)S(1)}, f32[2048]{0:T(1024)S(1)}) fusion(f32[2048,1024]{0,1:T(8,128)} %get-tuple-element.14, s32[2048]{0:T(1024)S(1)} %copy-done, s32[1024]{0:T(1024)S(1)} %iota_add_fusion, f32[2048]{0:T(1024)S(1)} %convert_element_type.17), kind=kLoop, calls=%fused_computation.4 | loop fusion | flops 10481664 | bytes 8425472 | tf_op jit(solution)/shard_map/reduce_sum | solution.py:20
  126.4 40.0 %all-reduce = (f32[2048]{0:T(1024)S(1)}, f32[2048]{0:T(1024)S(1)}) all-reduce(f32[2048]{0:T(1024)S(1)} %get-tuple-element.5, f32[2048]{0:T(1024)S(1)} %get-tuple-element.4), channel_id=1, replica_groups=mesh['dp'=8,'mp'=4] {'dp','mp'}, use_global_device_ids=true, to_apply=%region_3.4 | all-reduce | flops 4096 | bytes 32768 | tf_op jit(solution)/shard_map/psum | solution.py:47
  166.5 0.6 subtract_reduce_fusion
  167.8 0.0 copy-done.1
  167.8 12.5 %divide_subtract_fusion = (f32[1024,768]{1,0:T(8,128)}, f32[1024,768]{1,0:T(8,128)}, f32[1024,768]{1,0:T(8,128)}) fusion(f32[1024,768]{1,0:T(8,128)S(1)} %copy-done.1, f32[1024,768]{1,0:T(8,128)} %param.8, f32[1024,768]{1,0:T(8,128)} %param.9, bf16[2048,768]{1,0:T(8,128)(2,1)} %all-gather.2.cloned.1.call-done, f32[2048,1024]{0,1:T(8,128)} %get-tuple-element.14, ...), kind=kOutput, calls=%fused_computation.12 | convolution fusion | flops 3240361984 | bytes 30429184 | tf_op jit(solution)/shard_map/rk,rd->kd/dot_general | solution.py:50
  (2 shorter events, 0.0 us)
Async XLA Ops:
  7.2 65.8 %all-gather.2.cloned.1.call-start = ((), (), s32[]{:S(2)}) async-start(), calls=%async_computation | async-start | bytes 3538944 | tf_op jit(solution)/shard_map/all_gather | solution.py:38
  7.9 113.8 %copy-start = (s32[2048]{0:T(1024)S(1)}, s32[2048]{0:T(1024)}, u32[]{:S(2)}) copy-start(s32[2048]{0:T(1024)} %param.6) | copy-start | bytes 24580
  121.7 46.1 %copy-start.1 = (f32[1024,768]{1,0:T(8,128)S(1)}, f32[1024,768]{1,0:T(8,128)}, u32[]{:S(2)}) copy-start(f32[1024,768]{1,0:T(8,128)} %param.7) | copy-start | bytes 9437188
Sparse Core Ops, SparseCore 0:
  10.2 62.7 all-gather.1
where the time goes:
time: 189 us; the launch traced here: 188 us
  blocking collectives  79.3 us (42%)
  waiting for transfers between devices  65.7 us (35%)
  matrix products  22.1 us (12%)
  between operations  15.8 us (8%)
  other arithmetic  5.35 us (3%)
    all_gather x1, waiting for transfers between devices, shards(): gathered = lax.all_gather(query_emb, 'dp', axis=0, tiled=True)  65 us
    psum x1, blocking collectives, shards(): lax.psum((local_mass, target_logit(logits, is_target)), ('dp', 'mp'))  40 us
    pmax x1, blocking collectives, shards(): lax.pmax(jnp.max(logits, axis=1).astype(jnp.bfloat16), ('dp', 'mp'))  39.2 us
    dot_general x1, matrix products, shards(): jnp.einsum('rk,rd->kd', weights, gathered, preferred_element_type=jnp.flo...  12.5 us
    dot_general x1, matrix products, shards(): jnp.einsum('rd,kd->rk', gathered, table_half, preferred_element_type=jnp....  9.52 us
    reduce_sum x1, other arithmetic, target_logit(): return jnp.sum(jnp.where(is_target, logits, jnp.zeros_like(logits)), axis=1)  4.74 us
  transfers between devices with their start and end apart: 1, of which 1 were waited for; matrix products, arithmetic and copies ran while one was open for 0% of the time, Pallas kernels for 0%

commit v1 on v0

v1 whole, which is shorter than its diff:
```python
import functools

import jax
import jax.numpy as jnp
from jax import lax
from jax.experimental import pallas as pl
from jax.experimental.pallas import tpu as pltpu
from jax.sharding import PartitionSpec as P

beta_first = 0.9
beta_second = 0.95
learn_rate = 0.01
epsilon = 1e-08

MESH = pl.DeviceIdType.MESH


def adam_update(centroids, first_moment, second_moment, gradient):
    new_first = beta_first * first_moment + (1.0 - beta_first) * gradient
    new_second = beta_second * second_moment + (1.0 - beta_second) * gradient * gradient
    new_centroids = centroids - learn_rate * new_first / (jnp.sqrt(new_second) + epsilon)
    return (new_centroids, new_first, new_second)


def merge_stages(count_dp, count_mp):
    bits = [("mp", 1 << b) for b in range(count_mp.bit_length() - 1)]
    bits += [("dp", 1 << b) for b in range(count_dp.bit_length() - 1)]
    stages = [bits[:1]]
    for at in range(1, len(bits), 2):
        stages.append(bits[at : at + 2])
    return [
        [stage[:1]] if len(stage) == 1 else [stage[:1], stage[1:], stage] for stage in stages
    ]


def flip(index, bit):
    return index + (1 - 2 * lax.rem(lax.div(index, bit), 2)) * bit


def log_add(values):
    top = functools.reduce(jnp.maximum, values)
    terms = [jnp.exp(value - top) for value in values]
    while len(terms) > 1:
        terms = [terms[i] + terms[i + 1] for i in range(0, len(terms), 2)]
    return top + jnp.log(terms[0])


def plain_add(terms):
    while len(terms) > 1:
        terms = [terms[i] + terms[i + 1] for i in range(0, len(terms), 2)]
    return terms[0]


def kernel(
    n,
    count_mp,
    stages,
    q_ref,
    pos_ref,
    cent_ref,
    grad_ref,
    loss_ref,
    rows_all,
    logits,
    cent,
    table,
    weights,
    stats,
    landed,
    cent_sem,
    ring_send,
    ring_recv,
    pair_send,
    pair_recv,
    stat_send,
    stat_recv,
):
    R, D = q_ref.shape
    K = cent_ref.shape[0]
    half = R // 2
    piece = half // 2
    dp = lax.axis_index("dp")
    mp = lax.axis_index("mp")
    core = lax.rem(mp, 2)
    other = mp + 1 - 2 * core
    odd = lax.rem(dp, 2)
    place = (1 - odd) * lax.div(dp, 2) + odd * (n - 1 - lax.div(dp, 2))

    def at_place(p):
        back = lax.div(p, n // 2)
        return (1 - back) * 2 * p + back * (2 * (n - 1 - p) + 1)

    right = at_place(lax.rem(place + 1, n))
    left = at_place(lax.rem(place + n - 1, n))

    cent_copy = pltpu.make_async_copy(cent_ref, cent, cent_sem)
    cent_copy.start()

    def peer(mask):
        ids = {"dp": dp, "mp": mp}
        for axis, bit in mask:
            ids[axis] = flip(ids[axis], bit)
        return ids

    greeted = [{"dp": left, "mp": mp}, {"dp": right, "mp": mp}]
    greeted += [peer(mask) for stage in stages for mask in stage]
    barrier = pltpu.get_barrier_semaphore()
    for device in greeted:
        pl.semaphore_signal(barrier, inc=1, device_id=device, device_id_type=MESH)
    pl.semaphore_wait(barrier, len(greeted))

    def rows(origin, which, p):
        start = pl.multiple_of(origin * R + which * half + p * piece, piece)
        return rows_all.at[pl.ds(start, piece)]

    def ring_copy(src, origin, j, p, target):
        return pltpu.make_async_remote_copy(
            src_ref=src,
            dst_ref=rows(origin, core, p),
            send_sem=ring_send.at[j, p],
            recv_sem=ring_recv.at[j, p],
            device_id={"dp": target, "mp": mp},
            device_id_type=MESH,
        )

    def pair_copy(origin, j, p, which):
        block = rows(origin, which, p)
        return pltpu.make_async_remote_copy(
            src_ref=block,
            dst_ref=block,
            send_sem=pair_send.at[j, p],
            recv_sem=pair_recv.at[j, p],
            device_id={"dp": dp, "mp": other},
            device_id_type=MESH,
        )

    for p in range(2):
        own = q_ref.at[pl.ds(pl.multiple_of(core * half + p * piece, piece), piece)]
        ring_copy(own, dp, 1, p, right).start()
        ring_copy(own, dp, 2, p, left).start()

    base = (dp * count_mp + mp) * K
    first = stats.at[0]
    first[pl.ds(n, 8), :] = jnp.zeros((8, R), jnp.float32)

    def is_target(origin, start, size):
        local = pos_ref[pl.ds(origin, 1), :] - (base + start)
        return lax.broadcasted_iota(jnp.int32, (size, R), 0) == local

    step_rows = min(K, 256)

    def forward(origin):
        block = rows_all[pl.ds(pl.multiple_of(origin * R, R), R), :]
        found = lax.dot_general(
            table[...], block, (((1,), (1,)), ((), ())), preferred_element_type=jnp.float32
        )
        logits[origin] = found
        peak = jnp.max(found, axis=0, keepdims=True)
        mass = jnp.zeros((1, R), jnp.float32)
        target = jnp.zeros((1, R), jnp.float32)
        for start in range(0, K, step_rows):
            part = logits[origin, pl.ds(start, step_rows), :]
            mass += jnp.sum(jnp.exp(part - peak), axis=0, keepdims=True)
            target += jnp.sum(
                jnp.where(is_target(origin, start, step_rows), part, 0.0), axis=0, keepdims=True
            )
        first[pl.ds(origin, 1), :] = peak + jnp.log(mass)
        first[pl.ds(n, 1), :] += target

    rows_all[pl.ds(pl.multiple_of(dp * R, R), R), :] = q_ref[...]
    cent_copy.wait()
    for start in range(0, K, step_rows):
        table[pl.ds(start, step_rows), :] = cent[pl.ds(start, step_rows), :].astype(jnp.bfloat16)

    forward(dp)
    far = n // 2

    def ring_step(d, carry):
        from_left = at_place(lax.rem(place - d + n, n))
        from_right = at_place(lax.rem(place + d, n))
        jl, jr = 2 * d - 1, 2 * d
        for p in range(2):
            block = rows(from_left, core, p)
            ring_copy(block, from_left, jl, p, right).wait_recv()
            onward = ring_copy(block, from_left, 2 * d + 1, p, right)
            if p == 0:
                onward.start()
            else:
                pl.when(d + 1 < far)(onward.start)
            pair_copy(from_left, jl, p, core).start()

            block = rows(from_right, core, p)
            ring_copy(block, from_right, jr, p, left).wait_recv()
            onward = ring_copy(
                block, from_right, 2 * d + 2 - p * lax.div(d + 1, far), p, left
            )
            if p == 1:
                onward.start()
            else:
                pl.when(d + 1 < far)(onward.start)
            pair_copy(from_right, jr, p, core).start()
        for p in range(2):
            pair_copy(from_left, jl, p, 1 - core).wait_recv()
            pair_copy(from_right, jr, p, 1 - core).wait_recv()
        forward(from_left)
        forward(from_right)
        return carry

    lax.fori_loop(1, far, ring_step, 0)

    last = at_place(lax.rem(place + far, n))
    for p in range(2):
        ring_copy(rows(last, core, p), last, n - 1, p, right).wait_recv()
        pair_copy(last, n - 1, p, core).start()
    for p in range(2):
        pair_copy(last, n - 1, p, 1 - core).wait_recv()
    forward(last)

    slot = 0
    for at, stage in enumerate(stages):
        copies = []
        for mask in stage:
            copies.append(
                pltpu.make_async_remote_copy(
                    src_ref=stats.at[at],
                    dst_ref=landed.at[slot],
                    send_sem=stat_send.at[slot],
                    recv_sem=stat_recv.at[slot],
                    device_id=peer(mask),
                    device_id_type=MESH,
                )
            )
            copies[-1].start()
            slot += 1
        for copy in copies:
            copy.wait_recv()
        held = [stats.at[at]] + [landed.at[slot - len(stage) + i] for i in range(len(stage))]
        merged = stats.at[at + 1]
        merged[pl.ds(0, n), :] = log_add([ref[pl.ds(0, n), :] for ref in held])
        merged[pl.ds(n, 8), :] = plain_add([ref[pl.ds(n, 8), :] for ref in held])
        for copy in copies:
            copy.wait_send()

    final = stats.at[len(stages)]
    loss = (jnp.sum(final[pl.ds(0, n), :]) - jnp.sum(final[pl.ds(n, 8), :])) * (1.0 / (n * R))
    loss_ref[...] = jnp.full(loss_ref.shape, loss, jnp.float32)

    chunk = weights.shape[0]

    def backward(i, carry):
        start = pl.multiple_of(i * chunk, chunk)
        for b in range(n):
            part = jnp.exp(logits[b, pl.ds(start, chunk), :] - final[pl.ds(b, 1), :])
            hit = is_target(b, start, chunk)
            weights[:, pl.ds(b * R, R)] = jnp.where(hit, part - 1.0, part).astype(jnp.bfloat16)
        grad_ref[pl.ds(start, chunk), :] = jnp.dot(
            weights[...], rows_all[...], preferred_element_type=jnp.float32
        )
        return carry

    lax.fori_loop(0, K // chunk, backward, 0)

    def drain(j, carry):
        for p in range(2):
            ring_copy(rows(dp, core, p), dp, j, p, right).wait_send()
            pair_copy(dp, j, p, core).wait_send()
        return carry

    lax.fori_loop(1, n, drain, 0)


def shards(query_emb, positive_list, centroids, first_moment, second_moment):
    n, count_mp = lax.axis_size("dp"), lax.axis_size("mp")
    R, D = query_emb.shape
    K = centroids.shape[0]
    stages = merge_stages(n, count_mp)
    slots = sum(len(stage) for stage in stages)
    chunk = min(K, 256)
    vmem = pl.BlockSpec(memory_space=pltpu.VMEM)
    gradient, loss = pl.pallas_call(
        functools.partial(kernel, n, count_mp, stages),
        out_shape=(
            jax.ShapeDtypeStruct((K, D), jnp.float32),
            jax.ShapeDtypeStruct((8, 128), jnp.float32),
        ),
        in_specs=[vmem, vmem, pl.BlockSpec(memory_space=pl.ANY)],
        out_specs=(vmem, vmem),
        scratch_shapes=[
            pltpu.VMEM((n * R, D), jnp.bfloat16),
            pltpu.VMEM((n, K, R), jnp.float32),
            pltpu.VMEM((K, D), jnp.float32),
            pltpu.VMEM((K, D), jnp.bfloat16),
            pltpu.VMEM((chunk, n * R), jnp.bfloat16),
            pltpu.VMEM((len(stages) + 1, n + 8, R), jnp.float32),
            pltpu.VMEM((slots, n + 8, R), jnp.float32),
            pltpu.SemaphoreType.DMA,
            pltpu.SemaphoreType.DMA((n, 2)),
            pltpu.SemaphoreType.DMA((n, 2)),
            pltpu.SemaphoreType.DMA((n, 2)),
            pltpu.SemaphoreType.DMA((n, 2)),
            pltpu.SemaphoreType.DMA((slots,)),
            pltpu.SemaphoreType.DMA((slots,)),
        ],
        compiler_params=pltpu.CompilerParams(
            collective_id=0, has_side_effects=True, vmem_limit_bytes=36 * 2**20
        ),
        cost_estimate=pl.CostEstimate(
            flops=4 * n * R * K * D, bytes_accessed=8 * K * D, transcendentals=2 * n * R * K
        ),
        name="gather_softmax_gradient",
    )(query_emb, positive_list.reshape(n, R), centroids)
    new_centroids, new_first, new_second = adam_update(
        centroids, first_moment, second_moment, gradient
    )
    return (new_centroids, new_first, new_second, loss[0, 0])


def solution(mesh):
    in_specs = (
        P("dp", None),
        P(),
        P(("dp", "mp"), None),
        P(("dp", "mp"), None),
        P(("dp", "mp"), None),
    )
    out_specs = (P(("dp", "mp"), None), P(("dp", "mp"), None), P(("dp", "mp"), None), P())
    return jax.shard_map(shards, mesh=mesh, in_specs=in_specs, out_specs=out_specs, check_vma=False)
```

time: 189 us -> 51.9 us (0.27)
  blocking collectives: 79.3 us -> 0 us
  waiting for transfers between devices: 65.7 us -> 0 us
  Pallas kernels: 0 us -> 42 us
  matrix products: 22.1 us -> 0 us
  between operations: 15.8 us -> 0.64 us
  local copies, waits for them, and re-layouts: 0.01 us -> 4.11 us
    all_gather x1 -> x0, waiting for transfers between devices: 65 us -> none  [shards(): gathered = lax.all_gather(query_emb, 'dp', axis=0, tiled=True)]
    pallas_call x0 -> x1, Pallas kernels: none -> 42 us  [shards(): pl.pallas_call(functools.partial(kernel, n, count_mp, stages), out_shape=...]
    psum x1 -> x0, blocking collectives: 40 us -> none  [shards(): lax.psum((local_mass, target_logit(logits, is_target)), ('dp', 'mp'))]
    pmax x1 -> x0, blocking collectives: 39.2 us -> none  [shards(): lax.pmax(jnp.max(logits, axis=1).astype(jnp.bfloat16), ('dp', 'mp'))]
    dot_general x2 -> x0, matrix products: 22.1 us -> none  [the longest x1 12.5 us: shards(): jnp.einsum('rk,rd->kd', weights, gathered, preferred_element_type=jnp.flo...]
    reduce_sum x2 -> x0, other arithmetic: 5.35 us -> none  [the longest x1 4.74 us: target_logit(): return jnp.sum(jnp.where(is_target, logits, jnp.zeros_like(logits)), axis=1)]
    sub x0 -> x1, other arithmetic: none -> 4.94 us  [adam_update(): centroids - learn_rate * new_first / (jnp.sqrt(new_second) + epsilon)]
    unnamed x4 -> x10, local copies, waits for them, and re-layouts: 0.01 us -> 2.9 us
  transfers between devices with their start and end apart: 1 -> 0, of which waited for: 1 -> 0; matrix products, arithmetic and copies ran while one was open for 0% -> 0% of each run, Pallas kernels for 0% -> 0%
where the time goes in v1:
time: 51.9 us; the launch traced here: 51.7 us
  Pallas kernels  42 us (81%)
  other arithmetic  4.94 us (10%)
  local copies, waits for them, and re-layouts  4.11 us (8%)
  between operations  0.64 us (1%)
    pallas_call x1, Pallas kernels, shards(): pl.pallas_call(functools.partial(kernel, n, count_mp, stages), out_shape=...  42 us
    sub x1, other arithmetic, adam_update(): centroids - learn_rate * new_first / (jnp.sqrt(new_second) + epsilon)  4.94 us
    unnamed x10, local copies, waits for them, and re-layouts  2.9 us

profile of v1, /device:TPU:0, one launch (start us, length us, event | category | flops | bytes accessed | tf_op | source)
XLA Modules:
  0.0 51.7 jit_solution(8168095506724678034)
XLA Ops:
  0.6 0.7 %reshape.11.pos_ref = s32[8,256]{1,0:T(8,128)S(1)} reshape(s32[2048]{0:T(1024)} %param.6) | data formatting | bytes 16384 | tf_op jit(solution)/shard_map/reshape | solution.py:311
  1.3 0.0 copy-start
  1.3 1.9 %copy-done = f32[1024,768]{1,0:T(8,128)S(1)} copy-done((f32[1024,768]{1,0:T(8,128)S(1)}, f32[1024,768]{1,0:T(8,128)}, u32[]{:S(2)}) %copy-start) | copy-done | bytes 3145752
  3.2 0.0 copy-start.2
  3.2 1.0 %copy-done.2 = bf16[256,768]{1,0:T(8,128)(2,1)S(1)} copy-done((bf16[256,768]{1,0:T(8,128)(2,1)S(1)}, bf16[256,768]{1,0:T(8,128)(2,1)}, u32[]{:S(2)}) %copy-start.2) | copy-done | bytes 393240
  4.2 0.0 copy-start.1
  4.2 0.0 copy-start.3
  4.2 0.0 copy-start.4
  4.2 42.0 %gather_softmax_gradient.1 = (f32[1024,768]{1,0:T(8,128)S(1)}, f32[8,128]{1,0:T(8,128)S(1)}) custom-call(bf16[256,768]{1,0:T(8,128)(2,1)S(1)} %copy-done.2, s32[8,256]{1,0:T(8,128)S(1)} %reshape.11.pos_ref, f32[1024,768]{1,0:T(8,128)S(1)} %copy-done), custom_call_target="tpu_custom_call" | custom-call | flops 6442450944 | bytes 6291456 | tf_op jit(solution)/shard_map/gather_softmax_gradient/pallas_call | solution.py:280
  46.2 0.5 slice.3
  46.7 0.0 copy-done.1
  46.7 0.0 copy-done.3
  46.7 0.0 copy-done.4
  46.8 4.9 %divide_subtract_fusion = (f32[1024,768]{1,0:T(8,128)}, f32[1024,768]{1,0:T(8,128)}, f32[1024,768]{1,0:T(8,128)}) fusion(f32[1024,768]{1,0:T(8,128)S(1)} %copy-done.1, f32[1024,768]{1,0:T(8,128)S(1)} %get-tuple-element.6, f32[1024,768]{1,0:T(8,128)S(1)} %copy-done.3, f32[1024,768]{1,0:T(8,128)S(1)} %copy-done.4), kind=kLoop, calls=%fused_computation.2 | loop fusion | flops 8650752 | bytes 22020096 | tf_op jit(solution)/shard_map/sub | solution.py:21
Async XLA Ops:
  1.3 1.9 %copy-start = (f32[1024,768]{1,0:T(8,128)S(1)}, f32[1024,768]{1,0:T(8,128)}, u32[]{:S(2)}) copy-start(f32[1024,768]{1,0:T(8,128)} %cent_ref.1) | copy-start | bytes 9437188
  3.2 1.0 %copy-start.2 = (bf16[256,768]{1,0:T(8,128)(2,1)S(1)}, bf16[256,768]{1,0:T(8,128)(2,1)}, u32[]{:S(2)}) copy-start(bf16[256,768]{1,0:T(8,128)(2,1)} %q_ref.1) | copy-start | bytes 1179652
  4.2 42.5 %copy-start.1 = (f32[1024,768]{1,0:T(8,128)S(1)}, f32[1024,768]{1,0:T(8,128)}, u32[]{:S(2)}) copy-start(f32[1024,768]{1,0:T(8,128)} %cent_ref.1) | copy-start | bytes 9437188
  4.2 42.5 %copy-start.3 = (f32[1024,768]{1,0:T(8,128)S(1)}, f32[1024,768]{1,0:T(8,128)}, u32[]{:S(2)}) copy-start(f32[1024,768]{1,0:T(8,128)} %param.8) | copy-start | bytes 9437188
  4.2 42.5 %copy-start.4 = (f32[1024,768]{1,0:T(8,128)S(1)}, f32[1024,768]{1,0:T(8,128)}, u32[]{:S(2)}) copy-start(f32[1024,768]{1,0:T(8,128)} %param.9) | copy-start | bytes 9437188

commit v2 on v1

--- a/solution.py
+++ b/solution.py
@@ -68,6 +68,7 @@
     stats,
     landed,
     cent_sem,
+    own_sem,
     ring_send,
     ring_recv,
     pair_send,
@@ -94,6 +95,9 @@
     left = at_place(lax.rem(place + n - 1, n))
 
     cent_copy = pltpu.make_async_copy(cent_ref, cent, cent_sem)
+    own_rows = rows_all.at[pl.ds(pl.multiple_of(dp * R, R), R)]
+    own_copy = pltpu.make_async_copy(q_ref, own_rows, own_sem)
+    own_copy.start()
     cent_copy.start()
 
     def peer(mask):
@@ -134,8 +138,9 @@
             device_id_type=MESH,
         )
 
+    own_copy.wait()
     for p in range(2):
-        own = q_ref.at[pl.ds(pl.multiple_of(core * half + p * piece, piece), piece)]
+        own = rows(dp, core, p)
         ring_copy(own, dp, 1, p, right).start()
         ring_copy(own, dp, 2, p, left).start()
 
@@ -167,7 +172,6 @@
         first[pl.ds(origin, 1), :] = peak + jnp.log(mass)
         first[pl.ds(n, 1), :] += target
 
-    rows_all[pl.ds(pl.multiple_of(dp * R, R), R), :] = q_ref[...]
     cent_copy.wait()
     for start in range(0, K, step_rows):
         table[pl.ds(start, step_rows), :] = cent[pl.ds(start, step_rows), :].astype(jnp.bfloat16)
@@ -277,13 +281,14 @@
     slots = sum(len(stage) for stage in stages)
     chunk = min(K, 256)
     vmem = pl.BlockSpec(memory_space=pltpu.VMEM)
+    hbm = pl.BlockSpec(memory_space=pltpu.HBM)
     gradient, loss = pl.pallas_call(
         functools.partial(kernel, n, count_mp, stages),
         out_shape=(
             jax.ShapeDtypeStruct((K, D), jnp.float32),
-            jax.ShapeDtypeStruct((8, 128), jnp.float32),
+            jax.ShapeDtypeStruct((1, 1), jnp.float32),
         ),
-        in_specs=[vmem, vmem, pl.BlockSpec(memory_space=pl.ANY)],
+        in_specs=[hbm, vmem, hbm],
         out_specs=(vmem, vmem),
         scratch_shapes=[
             pltpu.VMEM((n * R, D), jnp.bfloat16),
@@ -293,6 +298,7 @@
             pltpu.VMEM((chunk, n * R), jnp.bfloat16),
             pltpu.VMEM((len(stages) + 1, n + 8, R), jnp.float32),
             pltpu.VMEM((slots, n + 8, R), jnp.float32),
+            pltpu.SemaphoreType.DMA,
             pltpu.SemaphoreType.DMA,
             pltpu.SemaphoreType.DMA((n, 2)),
             pltpu.SemaphoreType.DMA((n, 2)),
@@ -308,7 +314,7 @@
             flops=4 * n * R * K * D, bytes_accessed=8 * K * D, transcendentals=2 * n * R * K
         ),
         name="gather_softmax_gradient",
-    )(query_emb, positive_list.reshape(n, R), centroids)
+    )(pltpu.with_memory_space_constraint(query_emb, pltpu.HBM), positive_list.reshape(n, R), pltpu.with_memory_space_constraint(centroids, pltpu.HBM))
     new_centroids, new_first, new_second = adam_update(
         centroids, first_moment, second_moment, gradient
     )

time: 51.9 us -> 50.7 us (0.977)
  local copies, waits for them, and re-layouts: 4.11 us -> 0.71 us
  between operations: 0.64 us -> 2.41 us
    unnamed x10 -> x6, local copies, waits for them, and re-layouts: 2.9 us -> 0.01 us
where the time goes in v2:
time: 50.7 us; the launch traced here: 50.5 us
  Pallas kernels  42.4 us (84%)
  other arithmetic  4.94 us (10%)
  between operations  2.41 us (5%)
  local copies, waits for them, and re-layouts  0.71 us (1%)
    pallas_call x1, Pallas kernels, shards(): pl.pallas_call(functools.partial(kernel, n, count_mp, stages), out_shape=...  42.4 us
    sub x1, other arithmetic, adam_update(): centroids - learn_rate * new_first / (jnp.sqrt(new_second) + epsilon)  4.94 us

profile of v2, /device:TPU:0, one launch (start us, length us, event | category | flops | bytes accessed | tf_op | source)
XLA Modules:
  0.0 50.5 jit_solution(9018645325438738450)
XLA Ops:
  0.6 0.7 %reshape.11.pos_ref = s32[8,256]{1,0:T(8,128)S(1)} reshape(s32[2048]{0:T(1024)} %param.6) | data formatting | bytes 16384 | tf_op jit(solution)/shard_map/reshape | solution.py:317
  1.3 0.0 copy-start
  1.3 0.0 copy-start.1
  1.3 0.0 copy-start.2
  1.3 42.4 %gather_softmax_gradient.1 = (f32[1024,768]{1,0:T(8,128)S(1)}, f32[1,1]{1,0:T(1,128)}) custom-call(bf16[256,768]{1,0:T(8,128)(2,1)} %q_ref.1, s32[8,256]{1,0:T(8,128)S(1)} %reshape.11.pos_ref, f32[1024,768]{1,0:T(8,128)} %cent_ref.1), custom_call_target="tpu_custom_call" | custom-call | flops 6442450944 | bytes 6291456 | tf_op jit(solution)/shard_map/gather_softmax_gradient/pallas_call | solution.py:285
  43.7 0.0 copy-done
  43.7 0.0 copy-done.1
  43.8 0.0 copy-done.2
  43.8 4.9 %divide_subtract_fusion = (f32[1024,768]{1,0:T(8,128)}, f32[1024,768]{1,0:T(8,128)}, f32[1024,768]{1,0:T(8,128)}) fusion(f32[1024,768]{1,0:T(8,128)S(1)} %copy-done, f32[1024,768]{1,0:T(8,128)S(1)} %get-tuple-element.6, f32[1024,768]{1,0:T(8,128)S(1)} %copy-done.1, f32[1024,768]{1,0:T(8,128)S(1)} %copy-done.2), kind=kLoop, calls=%fused_computation.2 | loop fusion | flops 8650752 | bytes 22020096 | tf_op jit(solution)/shard_map/sub | solution.py:21
Async XLA Ops:
  1.3 42.4 %copy-start = (f32[1024,768]{1,0:T(8,128)S(1)}, f32[1024,768]{1,0:T(8,128)}, u32[]{:S(2)}) copy-start(f32[1024,768]{1,0:T(8,128)} %cent_ref.1) | copy-start | bytes 9437188
  1.3 42.4 %copy-start.1 = (f32[1024,768]{1,0:T(8,128)S(1)}, f32[1024,768]{1,0:T(8,128)}, u32[]{:S(2)}) copy-start(f32[1024,768]{1,0:T(8,128)} %param.8) | copy-start | bytes 9437188
  1.3 42.4 %copy-start.2 = (f32[1024,768]{1,0:T(8,128)S(1)}, f32[1024,768]{1,0:T(8,128)}, u32[]{:S(2)}) copy-start(f32[1024,768]{1,0:T(8,128)} %param.9) | copy-start | bytes 9437188

commit v3 on v2

--- a/solution.py
+++ b/solution.py
@@ -279,7 +279,7 @@
     K = centroids.shape[0]
     stages = merge_stages(n, count_mp)
     slots = sum(len(stage) for stage in stages)
-    chunk = min(K, 256)
+    chunk = min(K, 512)
     vmem = pl.BlockSpec(memory_space=pltpu.VMEM)
     hbm = pl.BlockSpec(memory_space=pltpu.HBM)
     gradient, loss = pl.pallas_call(

time: 50.7 us -> 50.4 us (level)
  no operation moved by 1% of the time
where the time goes in v3:
time: 50.4 us; the launch traced here: 50.1 us
  Pallas kernels  42.1 us (84%)
  other arithmetic  4.94 us (10%)
  between operations  2.41 us (5%)
  local copies, waits for them, and re-layouts  0.71 us (1%)
    pallas_call x1, Pallas kernels, shards(): pl.pallas_call(functools.partial(kernel, n, count_mp, stages), out_shape=...  42.1 us
    sub x1, other arithmetic, adam_update(): centroids - learn_rate * new_first / (jnp.sqrt(new_second) + epsilon)  4.94 us

profile of v3, /device:TPU:0, one launch (start us, length us, event | category | flops | bytes accessed | tf_op | source)
XLA Modules:
  0.0 50.1 jit_solution(3793000890515376845)
XLA Ops:
  0.6 0.7 %reshape.11.pos_ref = s32[8,256]{1,0:T(8,128)S(1)} reshape(s32[2048]{0:T(1024)} %param.6) | data formatting | bytes 16384 | tf_op jit(solution)/shard_map/reshape | solution.py:317
  1.3 0.0 copy-start
  1.3 0.0 copy-start.1
  1.3 0.0 copy-start.2
  1.3 42.1 %gather_softmax_gradient.1 = (f32[1024,768]{1,0:T(8,128)S(1)}, f32[1,1]{1,0:T(1,128)}) custom-call(bf16[256,768]{1,0:T(8,128)(2,1)} %q_ref.1, s32[8,256]{1,0:T(8,128)S(1)} %reshape.11.pos_ref, f32[1024,768]{1,0:T(8,128)} %cent_ref.1), custom_call_target="tpu_custom_call" | custom-call | flops 6442450944 | bytes 6291456 | tf_op jit(solution)/shard_map/gather_softmax_gradient/pallas_call | solution.py:285
  43.4 0.0 copy-done
  43.4 0.0 copy-done.1
  43.4 0.0 copy-done.2
  43.5 4.9 %divide_subtract_fusion = (f32[1024,768]{1,0:T(8,128)}, f32[1024,768]{1,0:T(8,128)}, f32[1024,768]{1,0:T(8,128)}) fusion(f32[1024,768]{1,0:T(8,128)S(1)} %copy-done, f32[1024,768]{1,0:T(8,128)S(1)} %get-tuple-element.6, f32[1024,768]{1,0:T(8,128)S(1)} %copy-done.1, f32[1024,768]{1,0:T(8,128)S(1)} %copy-done.2), kind=kLoop, calls=%fused_computation.2 | loop fusion | flops 8650752 | bytes 22020096 | tf_op jit(solution)/shard_map/sub | solution.py:21
Async XLA Ops:
  1.3 42.1 %copy-start = (f32[1024,768]{1,0:T(8,128)S(1)}, f32[1024,768]{1,0:T(8,128)}, u32[]{:S(2)}) copy-start(f32[1024,768]{1,0:T(8,128)} %cent_ref.1) | copy-start | bytes 9437188
  1.3 42.1 %copy-start.1 = (f32[1024,768]{1,0:T(8,128)S(1)}, f32[1024,768]{1,0:T(8,128)}, u32[]{:S(2)}) copy-start(f32[1024,768]{1,0:T(8,128)} %param.8) | copy-start | bytes 9437188
  1.3 42.1 %copy-start.2 = (f32[1024,768]{1,0:T(8,128)S(1)}, f32[1024,768]{1,0:T(8,128)}, u32[]{:S(2)}) copy-start(f32[1024,768]{1,0:T(8,128)} %param.9) | copy-start | bytes 9437188
